TPU v7x, 32 devices: a whole 2x2x4 slice. The times are simulated.
32 devices in a mesh: gx: 2 (over x), gy: 16 (over z, y, core).
Axes of the slice: x: 2, y: 2, z: 4, core: 2. Of those that a mesh axis runs over, the one named last changes fastest.
Arguments:
- right_side: float32 [262144], P(('gx', 'gy')), may hold values from -60 to 60
- reaction: float32 [262144], P(('gx', 'gy')), may hold values from 0.5 to 2
- cell_slots: int32 [125, 4096], P(None, ('gx', 'gy')), may hold values from 0 to 12543
- cell_level: int32 [4096], P(('gx', 'gy')), may hold values from 0 to 2
- con_masters: int32 [5, 8192], P(None, ('gx', 'gy')), may hold values from 0 to 12287
- con_rows: int32 [8192], P(('gx', 'gy')), may hold values from 0 to 9
- send_lists: int32 [8, 16384], P(None, ('gx', 'gy')), may hold values from 0 to 8191
Outputs:
- solution: float32 [262144], P(('gx', 'gy'))
- residual: float32 [262144], P(('gx', 'gy'))
Inputs may be any that keep to these rules, and one draw needn't show every extreme that they name: `cell_slots`: column block of rank d indexes d's local list: its 8192 owned unknowns, then 512 values from each of ranks d - 1, ..., d - 4, then from d + 1, ..., d + 4, then its 256 constrained values (rank d = 16 gx + gy). `cell_level`: A cell of level l has side 2^(-l). `con_masters`: slots among the same rank's owned and ghost values. `con_rows`: row of the interpolation table: 5 fine nodes on each half of a coarse edge. `send_lists`: row j of rank s lists s's owned unknowns that fill ghost block j of rank s + j + 1 (j < 4) or of rank s - (j - 3); rows without such a rank are unused.
All inputs are finite; a program needn't handle non-finite values.
Results may differ from a plain program's by a relative error of at most 0.0002.
Values sent between devices are 32-bit elements; how exact they have to be, the bound alone decides.
A program may use at most 64 MiB of HBM per device.

v0:
```python
import functools

import jax
import jax.numpy as jnp
import numpy as np
from jax import lax
from jax.experimental import pallas as pl
from jax.experimental.pallas import tpu as pltpu
from jax.sharding import PartitionSpec as P

ITERS = 3
LANES = 128
SUMS = 4
ROUNDS = 2
UNROLL = 8
MESH = pl.DeviceIdType.MESH


def lagrange(node_list, points):
    node_count = len(node_list)
    values = np.ones((len(points), node_count))
    derivs = np.zeros((len(points), node_count))
    for basis_node in range(node_count):
        for other_node in range(node_count):
            if other_node != basis_node:
                values[:, basis_node] = (
                    values[:, basis_node]
                    * (points - node_list[other_node])
                    / (node_list[basis_node] - node_list[other_node])
                )
        for skipped in range(node_count):
            if skipped != basis_node:
                product_term = np.ones(len(points)) / (node_list[basis_node] - node_list[skipped])
                for other_node in range(node_count):
                    if other_node != basis_node and other_node != skipped:
                        product_term = (
                            product_term
                            * (points - node_list[other_node])
                            / (node_list[basis_node] - node_list[other_node])
                        )
                derivs[:, basis_node] = derivs[:, basis_node] + product_term
    return (values, derivs)


def tables():
    gll_offset = np.sqrt(3.0 / 7.0)
    lobatto = np.array([0.0, (1.0 - gll_offset) / 2.0, 0.5, (1.0 + gll_offset) / 2.0, 1.0])
    inner_point = np.sqrt(5.0 - 2.0 * np.sqrt(10.0 / 7.0)) / 3.0
    outer_point = np.sqrt(5.0 + 2.0 * np.sqrt(10.0 / 7.0)) / 3.0
    inner_weight = (322.0 + 13.0 * np.sqrt(70.0)) / 900.0
    outer_weight = (322.0 - 13.0 * np.sqrt(70.0)) / 900.0
    points = np.array([-outer_point, -inner_point, 0.0, inner_point, outer_point])
    gauss_weights = np.array(
        [outer_weight, inner_weight, 128.0 / 225.0, inner_weight, outer_weight]
    )
    points = (points + 1.0) / 2.0
    gauss_weights = gauss_weights / 2.0
    shapes, slopes = lagrange(lobatto, points)
    fine_points = np.concatenate([lobatto / 2.0, (1.0 + lobatto) / 2.0])
    interp, unused_slopes = lagrange(lobatto, fine_points)
    quad_weights = np.kron(gauss_weights, np.kron(gauss_weights, gauss_weights))
    grad_x = np.kron(slopes, np.kron(shapes, shapes))
    grad_y = np.kron(shapes, np.kron(slopes, shapes))
    grad_z = np.kron(shapes, np.kron(shapes, slopes))
    stiffness = np.zeros((125, 125))
    for gradient in (grad_x, grad_y, grad_z):
        stiffness = stiffness + gradient.T @ (quad_weights[:, None] * gradient)
    return (interp.astype(np.float32), stiffness.astype(np.float32))


def round_up(value, step):
    return -(-value // step) * step


def split(value):
    high = value.astype(jnp.bfloat16)
    low = (value - high.astype(jnp.float32)).astype(jnp.bfloat16)
    return high, low


def kernel(
    shape,
    interp,
    *refs,
):
    inputs, refs = refs[:8], refs[8:]
    solution_ref, residual_ref = refs[:2]
    staged, refs = refs[2:10], refs[10:]
    right_ref, reaction_ref, cells_ref, level_ref, masters_ref, rows_ref, lists_ref, stiff_ref = staged
    (
    load_sem,
    own_table,
    ghost_table,
    onehot,
    lane_of,
    row_of,
    weights,
    cell_buf,
    own_acc,
    ghost_acc,
    out_src,
    out_dst,
    back_src,
    back_dst,
    part,
    first_buf,
    mid_part,
    second_buf,
    out_send,
    out_recv,
    back_send,
    back_recv,
    first_send,
    first_recv,
    second_send,
    second_recv,
    ) = refs
    loads = [
        pltpu.make_async_copy(source, target, load_sem.at[i])
        for i, (source, target) in enumerate(zip(inputs, staged))
    ]
    for load in loads:
        load.start()
    nx, ny = shape
    count = nx * ny
    me = lax.axis_index("gx") * ny + lax.axis_index("gy")

    def place(rank):
        return (lax.div(rank, ny), lax.rem(rank, ny))

    blocks, listed = lists_ref.shape
    half = blocks // 2
    offsets = [j + 1 for j in range(half)] + [-(j + 1) for j in range(half)]
    own_rows = right_ref.shape[0]
    block_rows = listed // LANES
    ghost_rows = blocks * block_rows
    local_rows = own_rows + ghost_rows
    con_rows = rows_ref.shape[0]
    far_rows = round_up(ghost_rows + con_rows, 16)
    nodes = masters_ref.shape[0]
    points = cells_ref.shape[0]
    cell_rows = round_up(points, 8)
    cell_groups = cell_rows // 8
    list_groups = ghost_rows // 8
    list_base = cell_groups
    con_base = cell_groups + list_groups
    near = 1
    while near * near < count:
        near *= 2
    far = count // near
    near_id, far_id = lax.rem(me, near), lax.div(me, near)

    def near_peer(step):
        return far_id * near + lax.rem(near_id + step, near)

    def far_peer(step):
        return lax.rem(far_id + step, far) * near + near_id

    def ring_peer(offset):
        return lax.rem(me + offset + count, count)

    barrier = pltpu.get_barrier_semaphore()
    peers = [ring_peer(offset) for offset in offsets]
    peers += [near_peer(step) for step in range(1, near)]
    peers += [far_peer(step) for step in range(1, far)]
    for peer in peers:
        pl.semaphore_signal(barrier, inc=1, device_id=place(peer), device_id_type=MESH)

    for load in loads:
        load.wait()
    lane_of[...] = jnp.zeros_like(lane_of)
    row_of[...] = jnp.full_like(row_of, -1)

    def put(at, slots):
        size = slots.shape[0]
        lane_of[at : at + size, :] = lax.rem(slots, LANES)
        row_of[at : at + size, :] = lax.div(slots, LANES)

    put(0, cells_ref[...])
    for j in range(blocks):
        for q in range(block_rows):
            put(list_base * 8 + j * block_rows + q, lists_ref[j : j + 1, q * LANES : (q + 1) * LANES])
    weights[...] = jnp.zeros_like(weights)
    for h in range(con_rows):
        put((con_base + h) * 8, masters_ref[:, h * LANES : (h + 1) * LANES])
        chosen = rows_ref[h : h + 1, :]
        for k in range(nodes):
            weight = jnp.zeros((1, LANES), jnp.float32)
            for t in range(interp.shape[0]):
                weight = jnp.where(chosen == t, float(interp[t, k]), weight)
            weights[h * 8 + k : h * 8 + k + 1, :] = weight

    lane_iota = lax.broadcasted_iota(jnp.int32, (LANES, LANES), 0)

    def build(g, carry):
        lanes = lane_of[pl.ds(pl.multiple_of(g * 8, 8), 8), :]
        for i in range(8):
            hit = jnp.where(lanes[i : i + 1, :] == lane_iota, 1.0, 0.0)
            onehot[g, :, i * LANES : (i + 1) * LANES] = hit.astype(jnp.bfloat16)
        return carry

    lax.fori_loop(0, onehot.shape[0], build, 0)
    cell_buf[...] = jnp.zeros_like(cell_buf)
    scale = jnp.exp2(-level_ref[...].astype(jnp.float32))

    iota8 = lax.broadcasted_iota(jnp.int32, (8, LANES), 0)

    def gather(g, table, base, depth):
        stacked = table.shape[0] // 2
        pieces = [table[0:depth, :], table[stacked : stacked + depth, :]]
        left = table[...] if depth == stacked else jnp.concatenate(pieces, axis=0)
        spread = jnp.dot(left, onehot[g], preferred_element_type=jnp.float32)
        rows = row_of[pl.ds(pl.multiple_of(g * 8, 8), 8), :] - base
        found = []
        for i in range(8):
            wanted = jnp.broadcast_to(rows[i : i + 1, :], (8, LANES)) - iota8
            high = jnp.zeros((8, LANES), jnp.float32)
            low = high
            for k in range(depth // 8):
                hit = wanted == 8 * k
                at, cols = 8 * k, slice(i * LANES, (i + 1) * LANES)
                high = jnp.where(hit, spread[at : at + 8, cols], high)
                low = jnp.where(hit, spread[depth + at : depth + at + 8, cols], low)
            found.append(jnp.sum(high + low, axis=0, keepdims=True))
        return jnp.concatenate(found, axis=0)

    def scatter(g, values, base, depth):
        rows = row_of[pl.ds(pl.multiple_of(g * 8, 8), 8), :] - base
        high = values.astype(jnp.bfloat16).astype(jnp.float32)
        low = values - high
        row_iota = lax.broadcasted_iota(jnp.int32, (depth, LANES), 0)
        columns = []
        for i in range(8):
            hit = rows[i : i + 1, :] == row_iota
            upper = jnp.where(hit, high[i : i + 1, :], 0.0).astype(jnp.bfloat16)
            lower = jnp.where(hit, low[i : i + 1, :], 0.0).astype(jnp.bfloat16)
            columns.append(jnp.concatenate([upper, lower], axis=0))
        placed = jnp.concatenate(columns, axis=1)
        return lax.dot_general(
            placed, onehot[g], (((1,), (1,)), ((), ())), preferred_element_type=jnp.float32
        )

    def folded(both):
        depth = both.shape[0] // 2
        return both[0:depth] + both[depth : 2 * depth]

    def store(table, value):
        high, low = split(value)
        size = value.shape[0]
        table[0:size, :] = high
        table[size : 2 * size, :] = low

    def out_copy(turn, j):
        return pltpu.make_async_remote_copy(
            src_ref=out_src.at[turn, j],
            dst_ref=out_dst.at[turn, j],
            send_sem=out_send.at[turn, j],
            recv_sem=out_recv.at[turn, j],
            device_id=place(ring_peer(offsets[j])),
            device_id_type=MESH,
        )

    def back_copy(turn, j):
        return pltpu.make_async_remote_copy(
            src_ref=back_src.at[turn, j],
            dst_ref=back_dst.at[turn, j],
            send_sem=back_send.at[turn, j],
            recv_sem=back_recv.at[turn, j],
            device_id=place(ring_peer(-offsets[j])),
            device_id_type=MESH,
        )

    def near_copy(turn, step):
        return pltpu.make_async_remote_copy(
            src_ref=part.at[turn],
            dst_ref=first_buf.at[turn, near_id],
            send_sem=first_send.at[turn, step],
            recv_sem=first_recv.at[turn, step],
            device_id=place(near_peer(step)),
            device_id_type=MESH,
        )

    def far_copy(turn, step):
        return pltpu.make_async_remote_copy(
            src_ref=mid_part.at[turn],
            dst_ref=second_buf.at[turn, far_id],
            send_sem=second_send.at[turn, step],
            recv_sem=second_recv.at[turn, step],
            device_id=place(far_peer(step)),
            device_id_type=MESH,
        )

    def received(ref, turn, signs):
        rows = []
        for j in range(blocks):
            other = me + signs * offsets[j]
            inside = jnp.logical_and(other >= 0, other < count)
            rows.append(jnp.where(inside, ref[turn, j], 0.0))
        return jnp.concatenate(rows, axis=0)

    def group(g):
        return pl.ds(pl.multiple_of(g * 8, 8), 8)

    def apply(turn, vector, begin, middle):
        store(own_table, vector)
        per_group = 8 // block_rows
        for q in range(list_groups):
            found = gather(list_base + q, own_table, 0, own_rows)
            for r in range(per_group):
                j = q * per_group + r
                out_src[turn, j] = found[r * block_rows : (r + 1) * block_rows]
        if turn == 0:
            pl.semaphore_wait(barrier, len(peers))
        for j in range(blocks):
            out_copy(turn, j).start()

        def take_own(g, carry):
            cell_buf[group(g), :] = gather(g, own_table, 0, own_rows)
            return carry

        lax.fori_loop(0, cell_groups, take_own, 0, unroll=UNROLL)
        con_own = [gather(con_base + h, own_table, 0, own_rows) for h in range(con_rows)]
        for j in range(blocks):
            out_copy(turn, j).wait()
        ghosts = received(out_dst, turn, -1)
        padding = jnp.zeros((far_rows - ghost_rows, LANES), jnp.float32)
        store(ghost_table, jnp.concatenate([ghosts, padding], axis=0))
        resolved = []
        for h in range(con_rows):
            found = con_own[h] + gather(con_base + h, ghost_table, own_rows, ghost_rows)
            resolved.append(jnp.sum(weights[8 * h : 8 * h + 8, :] * found, axis=0, keepdims=True))
        resolved.append(jnp.zeros((far_rows - ghost_rows - con_rows, LANES), jnp.float32))
        store(ghost_table, jnp.concatenate([ghosts] + resolved, axis=0))

        def take_far(g, carry):
            cell_buf[group(g), :] += gather(g, ghost_table, own_rows, far_rows)
            return carry

        lax.fori_loop(0, cell_groups, take_far, 0, unroll=UNROLL)
        nodal = cell_buf[...]
        contrib = scale * jnp.dot(
            stiff_ref[...],
            nodal,
            precision=lax.Precision.HIGHEST,
            preferred_element_type=jnp.float32,
        )
        cell_buf[...] = contrib
        weighted = reaction_ref[...] * vector
        energy = jnp.sum(nodal * contrib, axis=0, keepdims=True)
        energy = energy + jnp.sum(weighted * vector, axis=0, keepdims=True)
        begin(energy)
        ghost_acc[...] = jnp.zeros_like(ghost_acc)

        def give_far(g, carry):
            ghost_acc[...] += scatter(g, cell_buf[group(g), :], own_rows, far_rows)
            return carry

        lax.fori_loop(0, cell_groups, give_far, 0, unroll=UNROLL)
        summed = folded(ghost_acc[...])
        spread = summed[0:ghost_rows]
        shares = []
        for h in range(con_rows):
            at = ghost_rows + h
            shares.append(weights[8 * h : 8 * h + 8, :] * summed[at : at + 1])
            spread = spread + folded(scatter(con_base + h, shares[h], own_rows, ghost_rows))
        for j in range(blocks):
            back_src[turn, j] = spread[j * block_rows : (j + 1) * block_rows]
        for j in range(blocks):
            back_copy(turn, j).start()
        middle()
        own_acc[...] = jnp.zeros_like(own_acc)

        def give_own(g, carry):
            own_acc[...] += scatter(g, cell_buf[group(g), :], 0, own_rows)
            return carry

        lax.fori_loop(0, cell_groups, give_own, 0, unroll=UNROLL)
        both = own_acc[...]
        for h in range(con_rows):
            both = both + scatter(con_base + h, shares[h], 0, own_rows)
        for j in range(blocks):
            back_copy(turn, j).wait()
        values = received(back_dst, turn, 1)
        for q in range(list_groups):
            both = both + scatter(list_base + q, values[8 * q : 8 * q + 8], 0, own_rows)
        return folded(both) + weighted

    def dot(one, two):
        return jnp.sum(one * two, axis=0, keepdims=True)

    def sums_start(turn, parts):
        mine = jnp.concatenate(parts, axis=0)
        part[turn] = mine
        first_buf[turn, near_id] = mine
        for step in range(1, near):
            near_copy(turn, step).start()

    def sums_middle(turn):
        for step in range(1, near):
            near_copy(turn, step).wait()
        mine = first_buf[turn, 0]
        for k in range(1, near):
            mine = mine + first_buf[turn, k]
        mid_part[turn] = mine
        second_buf[turn, far_id] = mine
        for step in range(1, far):
            far_copy(turn, step).start()

    def sums_end(turn):
        for step in range(1, far):
            far_copy(turn, step).wait()
        total = second_buf[turn, 0]
        for k in range(1, far):
            total = total + second_buf[turn, k]
        total = jnp.sum(total, axis=1, keepdims=True)
        return [total[k : k + 1] for k in range(SUMS)]

    start = right_ref[...]
    first = apply(0, start, lambda energy: None, lambda: None)
    known = [dot(start, start), dot(start, first), dot(first, first)]
    second = apply(
        1,
        first,
        lambda energy: sums_start(0, known + [energy]),
        lambda: sums_middle(0),
    )
    m0, m1, m2, m3 = sums_end(0)
    step0 = m0 / m1
    norm1 = m0 - 2.0 * step0 * m1 + step0 * step0 * m2
    product1 = m1 - 2.0 * step0 * m2 + step0 * step0 * m3
    ratio1 = norm1 / m0
    step1 = norm1 / (product1 - ratio1 * norm1 / step0)
    residual = start - step0 * first
    applied = first - step0 * second
    direction = residual + ratio1 * start
    applied_dir = applied + ratio1 * first
    answer = step0 * start + step1 * direction
    residual = residual - step1 * applied_dir
    zero = jnp.zeros((1, LANES), jnp.float32)
    square = dot(residual, residual)
    applied = apply(
        2,
        residual,
        lambda energy: sums_start(1, [square, energy, zero, zero]),
        lambda: sums_middle(1),
    )
    norm2, product2, unused_a, unused_b = sums_end(1)
    ratio2 = norm2 / norm1
    step2 = norm2 / (product2 - ratio2 * norm2 / step1)
    solution_ref[...] = answer + step2 * (residual + ratio2 * direction)
    residual_ref[...] = residual - step2 * (applied + ratio2 * applied_dir)


def on_device(shape, right_side, reaction, cell_slots, cell_level, con_masters, con_rows, send_lists):
    interp, stiffness = tables()
    own = right_side.shape[0]
    own_rows = own // LANES
    blocks, listed = send_lists.shape
    block_rows = listed // LANES
    con_tiles = con_rows.shape[0] // LANES
    points = cell_slots.shape[0]
    cell_rows = round_up(points, 8)
    far_rows = round_up(blocks * block_rows + con_tiles, 16)
    groups = cell_rows // 8 + blocks * block_rows // 8 + con_tiles
    padded = np.zeros((cell_rows, cell_rows), np.float32)
    padded[:points, :points] = stiffness
    count = shape[0] * shape[1]
    near = 1
    while near * near < count:
        near *= 2
    far = count // near
    operands = [
        right_side.reshape(own_rows, LANES),
        reaction.reshape(own_rows, LANES),
        cell_slots,
        cell_level.reshape(1, -1),
        con_masters,
        con_rows.reshape(con_tiles, LANES),
        send_lists,
        jnp.asarray(padded),
    ]
    exchange = pltpu.VMEM((ITERS, blocks, block_rows, LANES), jnp.float32)
    tile = jax.ShapeDtypeStruct((own_rows, LANES), jnp.float32)
    answer, residual = pl.pallas_call(
        functools.partial(kernel, shape, interp),
        out_shape=(tile, tile),
        in_specs=[pl.BlockSpec(memory_space=pl.ANY)] * 8,
        out_specs=(pl.BlockSpec(memory_space=pltpu.VMEM),) * 2,
        scratch_shapes=[
            *[pltpu.VMEM(value.shape, value.dtype) for value in operands],
            pltpu.SemaphoreType.DMA((len(operands),)),
            pltpu.VMEM((2 * own_rows, LANES), jnp.bfloat16),
            pltpu.VMEM((2 * far_rows, LANES), jnp.bfloat16),
            pltpu.VMEM((groups, LANES, 8 * LANES), jnp.bfloat16),
            pltpu.VMEM((groups * 8, LANES), jnp.int32),
            pltpu.VMEM((groups * 8, LANES), jnp.int32),
            pltpu.VMEM((con_tiles * 8, LANES), jnp.float32),
            pltpu.VMEM((cell_rows, LANES), jnp.float32),
            pltpu.VMEM((2 * own_rows, LANES), jnp.float32),
            pltpu.VMEM((2 * far_rows, LANES), jnp.float32),
            exchange,
            exchange,
            exchange,
            exchange,
            pltpu.VMEM((ROUNDS, SUMS, LANES), jnp.float32),
            pltpu.VMEM((ROUNDS, near, SUMS, LANES), jnp.float32),
            pltpu.VMEM((ROUNDS, SUMS, LANES), jnp.float32),
            pltpu.VMEM((ROUNDS, far, SUMS, LANES), jnp.float32),
            pltpu.SemaphoreType.DMA((ITERS, blocks)),
            pltpu.SemaphoreType.DMA((ITERS, blocks)),
            pltpu.SemaphoreType.DMA((ITERS, blocks)),
            pltpu.SemaphoreType.DMA((ITERS, blocks)),
            pltpu.SemaphoreType.DMA((ROUNDS, near)),
            pltpu.SemaphoreType.DMA((ROUNDS, near)),
            pltpu.SemaphoreType.DMA((ROUNDS, far)),
            pltpu.SemaphoreType.DMA((ROUNDS, far)),
        ],
        compiler_params=pltpu.CompilerParams(
            collective_id=0, has_side_effects=True, vmem_limit_bytes=60 * 1024 * 1024
        ),
    )(*operands)
    return (answer.reshape(own), residual.reshape(own))


def solution(mesh):
    placed = (
        P(("gx", "gy")),
        P(("gx", "gy")),
        P(None, ("gx", "gy")),
        P(("gx", "gy")),
        P(None, ("gx", "gy")),
        P(("gx", "gy")),
        P(None, ("gx", "gy")),
    )
    return jax.shard_map(
        functools.partial(on_device, (mesh.shape["gx"], mesh.shape["gy"])),
        mesh=mesh,
        in_specs=placed,
        out_specs=(P(("gx", "gy")), P(("gx", "gy"))),
        check_vma=False,
    )
```

profile of v0, /device:TPU:0, one launch (start us, length us, event | category | flops | bytes accessed | tf_op | source)
XLA Modules:
  0.0 51.4 jit_solution(13296152997879005863)
XLA Ops:
  0.6 48.7 %shard_map.95 = (f32[64,128]{1,0:T(8,128)}, f32[64,128]{1,0:T(8,128)}) custom-call(f32[64,128]{1,0:T(8,128)} %bitcast.6, f32[64,128]{1,0:T(8,128)} %bitcast.7, s32[125,128]{1,0:T(8,128)} %refs_2_.1, s32[1,128]{1,0:T(1,128)} %bitcast.11, s32[5,256]{1,0:T(8,128)} %refs_4_.1, s32[2,128]{1,0:T(2,128)} %bitcast.10, s32[8,512]{1,0:T(8,128)} %refs_6_.1, ...), custom_call_target="tpu_custom_call" | custom-call | tf_op jit(solution)/shard_map/pallas_call | solution.py:484
  49.3 0.0 copy-start
  49.4 1.4 %copy.12 = f32[8192]{0:T(1024)} copy(f32[8192]{0:T(1024)} %bitcast.9) | data formatting | bytes 65536
  50.7 0.0 copy-done
  50.7 0.6 %copy.13 = f32[8192]{0:T(1024)} copy(f32[8192]{0:T(1024)S(1)} %bitcast.8) | data formatting | bytes 65536
Async XLA Ops:
  49.3 1.4 %copy-start = (f32[64,128]{1,0:T(8,128)S(1)}, f32[64,128]{1,0:T(8,128)}, u32[]{:S(2)}) copy-start(f32[64,128]{1,0:T(8,128)} %get-tuple-element.5) | copy-start | bytes 98308
where the time goes:
time: 51.6 us; the launch traced here: 51.4 us
  Pallas kernels  48.7 us (94%)
  local copies, waits for them, and re-layouts  2 us (4%)
  between operations  0.65 us (1%)
    pallas_call x1, Pallas kernels, on_device(): pl.pallas_call(functools.partial(kernel, shape, interp), out_shape=(tile,...  48.7 us
    unnamed x4, local copies, waits for them, and re-layouts  2 us

commit v1 on v0

v1 whole, which is shorter than its diff:
```python
import functools

import jax
import jax.numpy as jnp
import numpy as np
from jax import lax
from jax.experimental import pallas as pl
from jax.experimental.pallas import tpu as pltpu
from jax.sharding import PartitionSpec as P

ITERS = 3
LANES = 128
SUMS = 4
ROUNDS = 2
UNROLL = 9
MESH = pl.DeviceIdType.MESH


def lagrange(node_list, points):
    node_count = len(node_list)
    values = np.ones((len(points), node_count))
    derivs = np.zeros((len(points), node_count))
    for basis_node in range(node_count):
        for other_node in range(node_count):
            if other_node != basis_node:
                values[:, basis_node] = (
                    values[:, basis_node]
                    * (points - node_list[other_node])
                    / (node_list[basis_node] - node_list[other_node])
                )
        for skipped in range(node_count):
            if skipped != basis_node:
                product_term = np.ones(len(points)) / (node_list[basis_node] - node_list[skipped])
                for other_node in range(node_count):
                    if other_node != basis_node and other_node != skipped:
                        product_term = (
                            product_term
                            * (points - node_list[other_node])
                            / (node_list[basis_node] - node_list[other_node])
                        )
                derivs[:, basis_node] = derivs[:, basis_node] + product_term
    return (values, derivs)


def tables():
    gll_offset = np.sqrt(3.0 / 7.0)
    lobatto = np.array([0.0, (1.0 - gll_offset) / 2.0, 0.5, (1.0 + gll_offset) / 2.0, 1.0])
    inner_point = np.sqrt(5.0 - 2.0 * np.sqrt(10.0 / 7.0)) / 3.0
    outer_point = np.sqrt(5.0 + 2.0 * np.sqrt(10.0 / 7.0)) / 3.0
    inner_weight = (322.0 + 13.0 * np.sqrt(70.0)) / 900.0
    outer_weight = (322.0 - 13.0 * np.sqrt(70.0)) / 900.0
    points = np.array([-outer_point, -inner_point, 0.0, inner_point, outer_point])
    gauss_weights = np.array(
        [outer_weight, inner_weight, 128.0 / 225.0, inner_weight, outer_weight]
    )
    points = (points + 1.0) / 2.0
    gauss_weights = gauss_weights / 2.0
    shapes, slopes = lagrange(lobatto, points)
    fine_points = np.concatenate([lobatto / 2.0, (1.0 + lobatto) / 2.0])
    interp, unused_slopes = lagrange(lobatto, fine_points)
    quad_weights = np.kron(gauss_weights, np.kron(gauss_weights, gauss_weights))
    grad_x = np.kron(slopes, np.kron(shapes, shapes))
    grad_y = np.kron(shapes, np.kron(slopes, shapes))
    grad_z = np.kron(shapes, np.kron(shapes, slopes))
    stiffness = np.zeros((125, 125))
    for gradient in (grad_x, grad_y, grad_z):
        stiffness = stiffness + gradient.T @ (quad_weights[:, None] * gradient)
    return (interp.astype(np.float32), stiffness.astype(np.float32))


def round_up(value, step):
    return -(-value // step) * step


def split(value):
    high = value.astype(jnp.bfloat16)
    low = (value - high.astype(jnp.float32)).astype(jnp.bfloat16)
    return high, low


def kernel(
    shape,
    interp,
    *refs,
):
    inputs, refs = refs[:8], refs[8:]
    answer_ref, ahead_ref, residual_ref, applied_ref, step_ref = refs[:5]
    staged, refs = refs[5:13], refs[13:]
    right_ref, reaction_ref, cells_ref, level_ref, masters_ref, rows_ref, lists_ref, stiff_ref = staged
    (
    load_sem,
    own_values,
    own_table,
    onehot,
    lane_of,
    row_of,
    weights,
    cell_buf,
    own_acc,
    far_acc,
    con_acc,
    out_src,
    out_dst,
    back_src,
    back_dst,
    part,
    first_buf,
    mid_part,
    second_buf,
    out_send,
    out_recv,
    back_send,
    back_recv,
    first_send,
    first_recv,
    second_send,
    second_recv,
    ) = refs
    loads = [
        pltpu.make_async_copy(source, target, load_sem.at[i])
        for i, (source, target) in enumerate(zip(inputs, staged))
    ]
    order = [0, 6, 2, 4, 5, 3, 1, 7]
    for i in order:
        loads[i].start()
    nx, ny = shape
    count = nx * ny
    inner = lax.axis_index("gy")
    me = lax.axis_index("gx") * ny + inner
    upper = lax.div(2 * inner, ny)

    def place(rank):
        return (lax.div(rank, ny), lax.rem(rank, ny))

    blocks, listed = lists_ref.shape
    half = blocks // 2
    own_rows = right_ref.shape[0]
    block_rows = listed // LANES
    ghost_rows = blocks * block_rows
    side_rows = half * block_rows
    con_rows = rows_ref.shape[0]
    con_pad = round_up(con_rows, 8)
    far_rows = ghost_rows + con_pad
    nodes = masters_ref.shape[0]
    points = cells_ref.shape[0]
    cell_rows = round_up(points, 8)
    cell_groups = cell_rows // 8
    list_groups = ghost_rows // 8
    side_groups = list_groups // 2
    per_group = 8 // block_rows
    con_base = cell_groups
    work_groups = cell_groups + con_rows
    list_base = work_groups
    near, far = phases(count)
    near_id, far_id = lax.rem(me, near), lax.div(me, near)
    sent_first = 1 - upper

    def offset(side, k):
        return (k + 1) * (1 - 2 * side)

    def near_peer(step):
        return far_id * near + lax.rem(near_id + step, near)

    def far_peer(step):
        return lax.rem(far_id + step, far) * near + near_id

    def ring_peer(distance):
        return lax.rem(me + distance + count, count)

    barrier = pltpu.get_barrier_semaphore()
    peers = [ring_peer(offset(side, k)) for side in range(2) for k in range(half)]
    peers += [near_peer(step) for step in range(1, near)]
    peers += [far_peer(step) for step in range(1, far)]
    for peer in peers:
        pl.semaphore_signal(barrier, inc=1, device_id=place(peer), device_id_type=MESH)

    def put(at, slots, shown):
        size = slots.shape[0]
        for copy in range(2 * ITERS):
            lane_of[copy, at : at + size, :] = lax.rem(slots, LANES)
        row_of[at : at + size, :] = jnp.where(shown, lax.div(slots, LANES), -1)

    def held(slots):
        rows = lax.div(slots, LANES) - own_rows
        shown = jnp.full(slots.shape, True)
        for side in range(2):
            for k in range(half):
                other = me - offset(side, k)
                low = (side * half + k) * block_rows
                outside = jnp.logical_or(other < 0, other >= count)
                hidden = jnp.logical_and(rows >= low, rows < low + block_rows)
                shown = jnp.logical_and(shown, jnp.logical_not(jnp.logical_and(hidden, outside)))
        return shown

    lane_iota = lax.broadcasted_iota(jnp.int32, (LANES, LANES), 0)

    def build(g, carry):
        lanes = lane_of[0, pl.ds(pl.multiple_of(g * 8, 8), 8), :]
        for i in range(8):
            hit = jnp.where(lanes[i : i + 1, :] == lane_iota, 1.0, 0.0)
            onehot[g, :, i * LANES : (i + 1) * LANES] = hit.astype(jnp.bfloat16)
        return carry

    iota8 = lax.broadcasted_iota(jnp.int32, (8, LANES), 0)

    once = 1 + lax.div(inner, ny)

    def apart(work):
        def body(i, carry):
            work()
            return carry

        lax.fori_loop(0, once, body, 0)

    def group(g):
        return pl.ds(pl.multiple_of(g * 8, 8), 8)

    def gather(g, table):
        depth = table.shape[0] // 2
        spread = jnp.dot(table[...], onehot[g], preferred_element_type=jnp.float32)
        rows = row_of[group(g), :]
        found = []
        for i in range(8):
            wanted = jnp.broadcast_to(rows[i : i + 1, :], (8, LANES)) - iota8
            high = jnp.zeros((8, LANES), jnp.float32)
            low = high
            for k in range(depth // 8):
                hit = wanted == 8 * k
                at, cols = 8 * k, slice(i * LANES, (i + 1) * LANES)
                high = jnp.where(hit, spread[at : at + 8, cols], high)
                low = jnp.where(hit, spread[depth + at : depth + at + 8, cols], low)
            found.append(jnp.sum(high + low, axis=0, keepdims=True))
        return jnp.concatenate(found, axis=0)

    def pick(lanes, rows, lines, found):
        for k, line in enumerate(lines):
            moved = jnp.take_along_axis(
                jnp.broadcast_to(line, (8, LANES)), lanes, axis=1, mode="promise_in_bounds"
            )
            found = jnp.where(rows == k, moved, found)
        return found

    def parts_of(values):
        high = values.astype(jnp.bfloat16).astype(jnp.float32)
        return high, values - high

    def against(placed, g):
        return lax.dot_general(
            placed, onehot[g], (((1,), (1,)), ((), ())), preferred_element_type=jnp.float32
        )

    def scatter(g, values, base, depth):
        rows = row_of[group(g), :] - base
        high, low = parts_of(values)
        row_iota = lax.broadcasted_iota(jnp.int32, (depth, LANES), 0)
        columns = []
        for i in range(8):
            hit = rows[i : i + 1, :] == row_iota
            upper_part = jnp.where(hit, high[i : i + 1, :], 0.0).astype(jnp.bfloat16)
            lower_part = jnp.where(hit, low[i : i + 1, :], 0.0).astype(jnp.bfloat16)
            columns.append(jnp.concatenate([upper_part, lower_part], axis=0))
        return against(jnp.concatenate(columns, axis=1), g)

    def scatter_far(g, values):
        rows = row_of[group(g), :] - own_rows
        high, low = parts_of(values)
        row_iota = lax.broadcasted_iota(jnp.int32, (ghost_rows, LANES), 0)
        con_iota = lax.broadcasted_iota(jnp.int32, (2 * con_pad, LANES), 0)
        con_row = ghost_rows + lax.rem(con_iota, con_pad)
        columns = []
        for i in range(8):
            one = rows[i : i + 1, :]
            hit = one == row_iota
            con_hit = one == con_row
            top, bottom = high[i : i + 1, :], low[i : i + 1, :]
            both = jnp.where(con_iota < con_pad, top, bottom)
            columns.append(
                jnp.concatenate(
                    [
                        jnp.where(hit, top, 0.0).astype(jnp.bfloat16),
                        jnp.where(hit, bottom, 0.0).astype(jnp.bfloat16),
                        jnp.where(con_hit, both, 0.0).astype(jnp.bfloat16),
                    ],
                    axis=0,
                )
            )
        placed = jnp.concatenate(columns, axis=1)
        return lax.dot_general(
            onehot[g], placed, (((1,), (1,)), ((), ())), preferred_element_type=jnp.float32
        )

    def folded(both):
        depth = both.shape[0] // 2
        return both[0:depth] + both[depth : 2 * depth]

    def store(table, value):
        high, low = split(value)
        size = value.shape[0]
        table[0:size, :] = high
        table[size : 2 * size, :] = low

    def out_copy(turn, side, k):
        j = side * half + k
        return pltpu.make_async_remote_copy(
            src_ref=out_src.at[turn, j],
            dst_ref=out_dst.at[turn, j],
            send_sem=out_send.at[side],
            recv_sem=out_recv.at[side],
            device_id=place(ring_peer(offset(side, k))),
            device_id_type=MESH,
        )

    def back_copy(turn, side, k):
        j = side * half + k
        return pltpu.make_async_remote_copy(
            src_ref=back_src.at[turn, j],
            dst_ref=back_dst.at[turn, j],
            send_sem=back_send.at[side],
            recv_sem=back_recv.at[side],
            device_id=place(ring_peer(-offset(side, k))),
            device_id_type=MESH,
        )

    def near_copy(turn, step):
        return pltpu.make_async_remote_copy(
            src_ref=part.at[turn],
            dst_ref=first_buf.at[turn, near_id],
            send_sem=first_send.at[turn],
            recv_sem=first_recv.at[turn],
            device_id=place(near_peer(step)),
            device_id_type=MESH,
        )

    def far_copy(turn, step):
        return pltpu.make_async_remote_copy(
            src_ref=mid_part.at[turn],
            dst_ref=second_buf.at[turn, far_id],
            send_sem=second_send.at[turn],
            recv_sem=second_recv.at[turn],
            device_id=place(far_peer(step)),
            device_id_type=MESH,
        )

    out_ends = (out_src, out_dst, out_send, out_recv)
    back_ends = (back_src, back_dst, back_send, back_recv)

    def lists_of(turn, side):
        found = []
        lines = [own_values[r : r + 1, :] for r in range(own_rows)]
        for q in range(side_groups):
            at = group(list_base + side * side_groups + q)
            zero = jnp.zeros((8, LANES), jnp.float32)
            found.append(pick(lane_of[2 * turn, at, :], row_of[at, :], lines, zero))
        return found

    def send_lists(turn, side, found):
        for q in range(side_groups):
            for r in range(per_group):
                j = side * half + q * per_group + r
                out_src[turn, j] = found[q][r * block_rows : (r + 1) * block_rows]

    def arrived(turn, side, mixed):
        source = turn
        if mixed is not None:
            source = ITERS
            for k in range(half):
                j = side * half + k
                out_dst[source, j] = mixed(*[out_dst[t, j] for t in range(turn + 1)])
        return [
            out_dst[source, side * half + k, r : r + 1, :] for k in range(half) for r in range(block_rows)
        ]

    def settle(ref, sem):
        pltpu.make_async_copy(ref, ref, sem).wait()

    def finish(ends, turn, side):
        source, target, send_sem, recv_sem = ends
        some = pl.ds(side * half, half)
        settle(source.at[turn, some], send_sem.at[side])
        settle(target.at[turn, some], recv_sem.at[side])

    def begin_apply(turn, vector):
        own_values[...] = vector
        for side in (sent_first, upper):
            send_lists(turn, side, lists_of(turn, side))
            if turn == 0 and side is sent_first:
                pl.semaphore_wait(barrier, len(peers))
            for k in range(half):
                out_copy(turn, side, k).start()

    def apply(turn, vector, mixed, begin, middle):
        store(own_table, vector)

        def take_own(g, carry):
            cell_buf[group(g), :] = gather(g, own_table)
            return carry

        lax.fori_loop(0, work_groups, take_own, 0, unroll=UNROLL)

        finish(out_ends, turn, sent_first)
        early, late = sent_first, upper
        lines = arrived(turn, early, mixed)
        base = own_rows + early * side_rows
        for g in range(work_groups):
            at = slice(8 * g, 8 * g + 8)
            cell_buf[at, :] = pick(lane_of[2 * turn, at, :], row_of[at, :] - base, lines, cell_buf[at, :])

        finish(out_ends, turn, late)
        lines = arrived(turn, late, mixed)
        base = own_rows + late * side_rows
        resolved = []
        for h in range(con_rows):
            at, to = slice(8 * (con_base + h), 8 * (con_base + h) + 8), slice(8 * h, 8 * h + 8)
            found = pick(lane_of[2 * turn + 1, at, :], row_of[at, :] - base, lines, cell_buf[at, :])
            resolved.append(jnp.sum(weights[to, :] * found, axis=0, keepdims=True))
        found = []
        for g in range(cell_groups):
            at = slice(8 * g, 8 * g + 8)
            found.append(pick(lane_of[2 * turn + 1, at, :], row_of[at, :] - base, lines, cell_buf[at, :]))
        for g in range(cell_groups):
            at = slice(8 * g, 8 * g + 8)
            rows = row_of[at, :] - (own_rows + ghost_rows)
            found[g] = pick(lane_of[2 * turn + 1, at, :], rows, resolved, found[g])
        nodal = jnp.concatenate(found, axis=0)
        contrib = scale * jnp.dot(
            stiff_ref[...],
            nodal,
            precision=lax.Precision.HIGHEST,
            preferred_element_type=jnp.float32,
        )
        cell_buf[0:cell_rows, :] = contrib
        weighted = reaction_ref[...] * vector
        energy = jnp.sum(nodal * contrib, axis=0, keepdims=True)
        energy = energy + jnp.sum(weighted * vector, axis=0, keepdims=True)
        begin(energy)

        far_acc[...] = jnp.zeros_like(far_acc)

        def give_far(g, carry):
            far_acc[...] += scatter_far(g, cell_buf[group(g), :])
            return carry

        lax.fori_loop(0, cell_groups, give_far, 0, unroll=8)
        total = jnp.transpose(far_acc[...])
        spread = total[0:ghost_rows] + total[ghost_rows : 2 * ghost_rows]
        summed = folded(total[2 * ghost_rows : 2 * far_rows])
        for h in range(con_rows):
            shares = weights[8 * h : 8 * h + 8, :] * summed[h : h + 1]
            cell_buf[8 * (con_base + h) : 8 * (con_base + h) + 8, :] = shares

        def give_con():
            total = jnp.zeros((2 * ghost_rows, LANES), jnp.float32)
            for h in range(con_rows):
                values = cell_buf[8 * (con_base + h) : 8 * (con_base + h) + 8, :]
                total = total + scatter(con_base + h, values, own_rows, ghost_rows)
            con_acc[...] = total

        apart(give_con)
        spread = spread + folded(con_acc[...])
        for j in range(blocks):
            back_src[turn, j] = spread[j * block_rows : (j + 1) * block_rows]
        for side in (late, early):
            for k in range(half):
                back_copy(turn, side, k).start()
        middle()
        own_acc[...] = jnp.zeros_like(own_acc)

        def give_own(g, carry):
            own_acc[...] += scatter(g, cell_buf[group(g), :], 0, own_rows)
            return carry

        lax.fori_loop(0, work_groups, give_own, 0, unroll=UNROLL)
        for side in (late, early):
            finish(back_ends, turn, side)

            def give_list(side=side):
                both = own_acc[...]
                for q in range(side_groups):
                    j = side * half + q * per_group
                    values = jnp.concatenate([back_dst[turn, j + r] for r in range(per_group)], axis=0)
                    both = both + scatter(list_base + side * side_groups + q, values, 0, own_rows)
                own_acc[...] = both

            apart(give_list)
        both = own_acc[...]
        return folded(both) + weighted

    def dot(one, two):
        return jnp.sum(one * two, axis=0, keepdims=True)

    lane = lax.broadcasted_iota(jnp.int32, (1, LANES), 1)
    width = LANES // SUMS

    def sums_start(turn, parts):
        total = jnp.sum(jnp.concatenate(parts, axis=0), axis=1, keepdims=True)
        mine = jnp.zeros((1, LANES), jnp.float32)
        for k in range(len(parts)):
            mine = jnp.where(lax.div(lane, width) == k, total[k : k + 1], mine)
        part[turn] = mine
        first_buf[turn, near_id] = mine

    def sums_send(turn):
        for step in range(1, near):
            near_copy(turn, step).start()

    def near_total(turn):
        others = pl.ds(0, near - 1)
        settle(first_buf.at[turn, others], first_send.at[turn])
        settle(first_buf.at[turn, others], first_recv.at[turn])
        mine = first_buf[turn, 0]
        for k in range(1, near):
            mine = mine + first_buf[turn, k]
        return mine

    def sums_middle(turn):
        sums_send(turn)
        if far == 1:
            return
        mine = near_total(turn)
        mid_part[turn] = mine
        second_buf[turn, far_id] = mine
        for step in range(1, far):
            far_copy(turn, step).start()

    def sums_end(turn):
        if far == 1:
            total = near_total(turn)
        else:
            others = pl.ds(0, far - 1)
            settle(second_buf.at[turn, others], second_send.at[turn])
            settle(second_buf.at[turn, others], second_recv.at[turn])
            total = second_buf[turn, 0]
            for k in range(1, far):
                total = total + second_buf[turn, k]
        return [total[:, k * width : k * width + 1] for k in range(SUMS)]

    loads[0].wait()
    loads[6].wait()
    for side in range(2):
        for k in range(half):
            j = side * half + k
            other = me + offset(side, k)
            inside = jnp.logical_and(other >= 0, other < count)
            for q in range(block_rows):
                at = list_base * 8 + j * block_rows + q
                put(at, lists_ref[j : j + 1, q * LANES : (q + 1) * LANES], inside)
    start = right_ref[...]
    begin_apply(0, start)
    for i in order[2:]:
        loads[i].wait()
    for copy in range(2 * ITERS):
        lane_of[copy, points:cell_rows, :] = jnp.zeros((cell_rows - points, LANES), jnp.int32)
    row_of[points:cell_rows, :] = jnp.full((cell_rows - points, LANES), -1, jnp.int32)
    slots = cells_ref[...]
    put(0, slots, held(slots))
    weights[...] = jnp.zeros_like(weights)
    for h in range(con_rows):
        at = (con_base + h) * 8
        for copy in range(2 * ITERS):
            lane_of[copy, at : at + 8, :] = jnp.zeros((8, LANES), jnp.int32)
        row_of[at : at + 8, :] = jnp.full((8, LANES), -1, jnp.int32)
        slots = masters_ref[:, h * LANES : (h + 1) * LANES]
        put(at, slots, held(slots))
        chosen = rows_ref[h : h + 1, :]
        for k in range(nodes):
            weight = jnp.zeros((1, LANES), jnp.float32)
            for t in range(interp.shape[0]):
                weight = jnp.where(chosen == t, float(interp[t, k]), weight)
            weights[h * 8 + k : h * 8 + k + 1, :] = weight
    lax.fori_loop(0, onehot.shape[0], build, 0)
    scale = jnp.exp2(-level_ref[...].astype(jnp.float32))

    first = apply(0, start, None, lambda energy: None, lambda: None)
    begin_apply(1, first)
    known = [dot(start, start), dot(start, first), dot(first, first)]
    second = apply(
        1,
        first,
        None,
        lambda energy: sums_start(0, known + [energy]),
        lambda: sums_middle(0),
    )
    begin_apply(2, second)
    m0, m1, m2, m3 = sums_end(0)
    step0 = m0 / m1
    norm1 = m0 - 2.0 * step0 * m1 + step0 * step0 * m2
    product1 = m1 - 2.0 * step0 * m2 + step0 * step0 * m3
    ratio1 = norm1 / m0
    step1 = norm1 / (product1 - ratio1 * norm1 / step0)

    def next_residual(zeroth, once, twice):
        before = zeroth - step0 * once
        along = once - step0 * twice + ratio1 * once
        return before, along, before - step1 * along

    before, applied_dir, residual = next_residual(start, first, second)
    direction = before + ratio1 * start
    answer = step0 * start + step1 * direction
    square = dot(residual, residual)
    applied = apply(
        2,
        residual,
        lambda *held: next_residual(*held)[2],
        lambda energy: sums_start(1, [square, energy]),
        lambda: sums_middle(1),
    )
    norm2, product2, unused_a, unused_b = sums_end(1)
    ratio2 = norm2 / norm1
    step2 = norm2 / (product2 - ratio2 * norm2 / step1)
    answer_ref[...] = answer
    ahead_ref[...] = residual + ratio2 * direction
    residual_ref[...] = residual
    applied_ref[...] = applied + ratio2 * applied_dir
    step_ref[...] = jnp.broadcast_to(step2, step_ref.shape)


def phases(count):
    if count <= 64:
        return count, 1
    near = 1
    while near * near < count:
        near *= 2
    return near, count // near


def on_device(shape, right_side, reaction, cell_slots, cell_level, con_masters, con_rows, send_lists):
    interp, stiffness = tables()
    own = right_side.shape[0]
    own_rows = own // LANES
    blocks, listed = send_lists.shape
    block_rows = listed // LANES
    con_tiles = con_rows.shape[0] // LANES
    points = cell_slots.shape[0]
    cell_rows = round_up(points, 8)
    far_rows = blocks * block_rows + round_up(con_tiles, 8)
    groups = cell_rows // 8 + blocks * block_rows // 8 + con_tiles
    padded = np.zeros((cell_rows, cell_rows), np.float32)
    padded[:points, :points] = stiffness
    count = shape[0] * shape[1]
    near, far = phases(count)
    operands = [
        right_side.reshape(own_rows, LANES),
        reaction.reshape(own_rows, LANES),
        cell_slots,
        cell_level.reshape(1, -1),
        con_masters,
        con_rows.reshape(con_tiles, LANES),
        send_lists,
        jnp.asarray(padded),
    ]
    exchange = pltpu.VMEM((ITERS, blocks, block_rows, LANES), jnp.float32)
    landing = pltpu.VMEM((ITERS + 1, blocks, block_rows, LANES), jnp.float32)
    tile = jax.ShapeDtypeStruct((own_rows, LANES), jnp.float32)
    line = jax.ShapeDtypeStruct((1, LANES), jnp.float32)
    answer, ahead, residual, applied, step = pl.pallas_call(
        functools.partial(kernel, shape, interp),
        out_shape=(tile, tile, tile, tile, line),
        in_specs=[pl.BlockSpec(memory_space=pl.ANY)] * 8,
        out_specs=(pl.BlockSpec(memory_space=pltpu.VMEM),) * 5,
        scratch_shapes=[
            *[pltpu.VMEM(value.shape, value.dtype) for value in operands],
            pltpu.SemaphoreType.DMA((len(operands),)),
            pltpu.VMEM((own_rows, LANES), jnp.float32),
            pltpu.VMEM((2 * own_rows, LANES), jnp.bfloat16),
            pltpu.VMEM((groups, LANES, 8 * LANES), jnp.bfloat16),
            pltpu.VMEM((2 * ITERS, groups * 8, LANES), jnp.int32),
            pltpu.VMEM((groups * 8, LANES), jnp.int32),
            pltpu.VMEM((con_tiles * 8, LANES), jnp.float32),
            pltpu.VMEM((cell_rows + 8 * con_tiles, LANES), jnp.float32),
            pltpu.VMEM((2 * own_rows, LANES), jnp.float32),
            pltpu.VMEM((LANES, 2 * far_rows), jnp.float32),
            pltpu.VMEM((2 * blocks * block_rows, LANES), jnp.float32),
            exchange,
            landing,
            exchange,
            exchange,
            pltpu.VMEM((ROUNDS, 1, LANES), jnp.float32),
            pltpu.VMEM((ROUNDS, near, 1, LANES), jnp.float32),
            pltpu.VMEM((ROUNDS, 1, LANES), jnp.float32),
            pltpu.VMEM((ROUNDS, far, 1, LANES), jnp.float32),
            pltpu.SemaphoreType.DMA((2,)),
            pltpu.SemaphoreType.DMA((2,)),
            pltpu.SemaphoreType.DMA((2,)),
            pltpu.SemaphoreType.DMA((2,)),
            pltpu.SemaphoreType.DMA((ROUNDS,)),
            pltpu.SemaphoreType.DMA((ROUNDS,)),
            pltpu.SemaphoreType.DMA((ROUNDS,)),
            pltpu.SemaphoreType.DMA((ROUNDS,)),
        ],
        compiler_params=pltpu.CompilerParams(
            collective_id=0, has_side_effects=True, vmem_limit_bytes=60 * 1024 * 1024
        ),
    )(*operands)
    scale = step[0, 0]
    return (
        (answer + scale * ahead).reshape(own),
        (residual - scale * applied).reshape(own),
    )


def solution(mesh):
    placed = (
        P(("gx", "gy")),
        P(("gx", "gy")),
        P(None, ("gx", "gy")),
        P(("gx", "gy")),
        P(None, ("gx", "gy")),
        P(("gx", "gy")),
        P(None, ("gx", "gy")),
    )
    return jax.shard_map(
        functools.partial(on_device, (mesh.shape["gx"], mesh.shape["gy"])),
        mesh=mesh,
        in_specs=placed,
        out_specs=(P(("gx", "gy")), P(("gx", "gy"))),
        check_vma=False,
    )
```

time: 51.6 us -> 46.9 us (0.909)
  Pallas kernels: 48.7 us -> 44 us
  other arithmetic: 0 us -> 1.47 us
  local copies, waits for them, and re-layouts: 2 us -> 0.62 us
    pallas_call x1, Pallas kernels: 48.7 us -> 44 us  [on_device(): pl.pallas_call(functools.partial(kernel, shape, interp), out_shape=(tile,...]
    reshape x0 -> x1, other arithmetic: none -> 1.47 us  [on_device(): (residual - scale * applied).reshape(own)]
    unnamed x4 -> x2, local copies, waits for them, and re-layouts: 2 us -> 0.62 us
where the time goes in v1:
time: 46.9 us; the launch traced here: 46.7 us
  Pallas kernels  44 us (94%)
  other arithmetic  1.47 us (3%)
  between operations  0.65 us (1%)
  local copies, waits for them, and re-layouts  0.62 us (1%)
    pallas_call x1, Pallas kernels, on_device(): pl.pallas_call(functools.partial(kernel, shape, interp), out_shape=(tile,...  44 us
    reshape x1, other arithmetic, on_device(): (residual - scale * applied).reshape(own)  1.47 us

profile of v1, /device:TPU:0, one launch (start us, length us, event | category | flops | bytes accessed | tf_op | source)
XLA Modules:
  0.0 46.7 jit_solution(17472386045966642240)
XLA Ops:
  0.6 44.0 %shard_map.95 = (f32[64,128]{1,0:T(8,128)}, f32[64,128]{1,0:T(8,128)}, f32[64,128]{1,0:T(8,128)}, f32[64,128]{1,0:T(8,128)}, f32[1,128]{1,0:T(1,128)}) custom-call(f32[64,128]{1,0:T(8,128)} %bitcast.10, f32[64,128]{1,0:T(8,128)} %bitcast.11, s32[125,128]{1,0:T(8,128)} %refs_2_.1, s32[1,128]{1,0:T(1,128)} %bitcast.13, s32[5,256]{1,0:T(8,128)} %refs_4_.1, ...), custom_call_target="tpu_custom_call" | custom-call | tf_op jit(solution)/shard_map/pallas_call | solution.py:655
  44.6 0.0 copy-start
  44.6 0.6 %copy-done = f32[1,128]{1,0:T(1,128)S(1)} copy-done((f32[1,128]{1,0:T(1,128)S(1)}, f32[1,128]{1,0:T(1,128)}, u32[]{:S(2)}) %copy-start) | copy-done | bytes 536
  45.2 1.5 %subtract_bitcast_fusion = (f32[8192]{0:T(1024)}, f32[8192]{0:T(1024)}) fusion(f32[64,128]{1,0:T(8,128)} %get-tuple-element.10, f32[64,128]{1,0:T(8,128)} %get-tuple-element.11, f32[]{:T(128)S(1)} %bitcast.14, f32[64,128]{1,0:T(8,128)} %get-tuple-element.7, f32[64,128]{1,0:T(8,128)} %get-tuple-element.9), kind=kLoop, calls=%fused_computation | loop fusion | flops 32768 | bytes 196612 | tf_op jit(solution)/shard_map/reshape | solution.py:697
Async XLA Ops:
  44.6 0.6 %copy-start = (f32[1,128]{1,0:T(1,128)S(1)}, f32[1,128]{1,0:T(1,128)}, u32[]{:S(2)}) copy-start(f32[1,128]{1,0:T(1,128)} %get-tuple-element.8) | copy-start | bytes 1540

commit v2 on v1

--- a/solution.py
+++ b/solution.py
@@ -154,6 +154,10 @@
     near, far = phases(count)
     near_id, far_id = lax.rem(me, near), lax.div(me, near)
     sent_first = 1 - upper
+    slow = min(1, half - 1)
+    slow_group = slow // per_group
+    group_order = [slow_group] + [q for q in range(side_groups) if q != slow_group]
+    block_order = [slow] + [k for k in range(half) if k != slow]
 
     def offset(side, k):
         return (k + 1) * (1 - 2 * side)
@@ -233,7 +237,7 @@
         return jnp.concatenate(found, axis=0)
 
     def pick(lanes, rows, lines, found):
-        for k, line in enumerate(lines):
+        for k, line in lines:
             moved = jnp.take_along_axis(
                 jnp.broadcast_to(line, (8, LANES)), lanes, axis=1, mode="promise_in_bounds"
             )
@@ -246,15 +250,18 @@
 
     def against(placed, g):
         return lax.dot_general(
-            placed, onehot[g], (((1,), (1,)), ((), ())), preferred_element_type=jnp.float32
+            placed,
+            onehot[g, :, 0 : placed.shape[1]],
+            (((1,), (1,)), ((), ())),
+            preferred_element_type=jnp.float32,
         )
 
-    def scatter(g, values, base, depth):
+    def scatter(g, values, base, depth, count=8):
         rows = row_of[group(g), :] - base
         high, low = parts_of(values)
         row_iota = lax.broadcasted_iota(jnp.int32, (depth, LANES), 0)
         columns = []
-        for i in range(8):
+        for i in range(count):
             hit = rows[i : i + 1, :] == row_iota
             upper_part = jnp.where(hit, high[i : i + 1, :], 0.0).astype(jnp.bfloat16)
             lower_part = jnp.where(hit, low[i : i + 1, :], 0.0).astype(jnp.bfloat16)
@@ -305,7 +312,7 @@
             src_ref=out_src.at[turn, j],
             dst_ref=out_dst.at[turn, j],
             send_sem=out_send.at[side],
-            recv_sem=out_recv.at[side],
+            recv_sem=out_recv.at[side, int(k == slow)],
             device_id=place(ring_peer(offset(side, k))),
             device_id_type=MESH,
         )
@@ -316,7 +323,7 @@
             src_ref=back_src.at[turn, j],
             dst_ref=back_dst.at[turn, j],
             send_sem=back_send.at[side],
-            recv_sem=back_recv.at[side],
+            recv_sem=back_recv.at[side, int(k == slow)],
             device_id=place(ring_peer(-offset(side, k))),
             device_id_type=MESH,
         )
@@ -344,49 +351,51 @@
     out_ends = (out_src, out_dst, out_send, out_recv)
     back_ends = (back_src, back_dst, back_send, back_recv)
 
-    def lists_of(turn, side):
-        found = []
-        lines = [own_values[r : r + 1, :] for r in range(own_rows)]
-        for q in range(side_groups):
-            at = group(list_base + side * side_groups + q)
-            zero = jnp.zeros((8, LANES), jnp.float32)
-            found.append(pick(lane_of[2 * turn, at, :], row_of[at, :], lines, zero))
-        return found
-
-    def send_lists(turn, side, found):
-        for q in range(side_groups):
-            for r in range(per_group):
-                j = side * half + q * per_group + r
-                out_src[turn, j] = found[q][r * block_rows : (r + 1) * block_rows]
-
-    def arrived(turn, side, mixed):
+    def list_values(turn, side, q):
+        lines = [(r, own_values[r : r + 1, :]) for r in range(own_rows)]
+        at = group(list_base + side * side_groups + q)
+        zero = jnp.zeros((8, LANES), jnp.float32)
+        found = pick(lane_of[2 * turn, at, :], row_of[at, :], lines, zero)
+        for r in range(per_group):
+            j = side * half + q * per_group + r
+            out_src[turn, j] = found[r * block_rows : (r + 1) * block_rows]
+
+    def arrived(turn, side, mixed, which):
         source = turn
         if mixed is not None:
             source = ITERS
-            for k in range(half):
+            for k in which:
                 j = side * half + k
                 out_dst[source, j] = mixed(*[out_dst[t, j] for t in range(turn + 1)])
         return [
-            out_dst[source, side * half + k, r : r + 1, :] for k in range(half) for r in range(block_rows)
+            (k * block_rows + r, out_dst[source, side * half + k, r : r + 1, :])
+            for k in which
+            for r in range(block_rows)
         ]
 
     def settle(ref, sem):
         pltpu.make_async_copy(ref, ref, sem).wait()
 
-    def finish(ends, turn, side):
-        source, target, send_sem, recv_sem = ends
-        some = pl.ds(side * half, half)
-        settle(source.at[turn, some], send_sem.at[side])
-        settle(target.at[turn, some], recv_sem.at[side])
+    def take_most(ends, turn, side):
+        if half > 1:
+            settle(ends[1].at[turn, pl.ds(side * half, half - 1)], ends[3].at[side, 0])
+
+    def take_slow(ends, turn, side):
+        settle(ends[1].at[turn, pl.ds(side * half, 1)], ends[3].at[side, 1])
+
+    def sent(ends, turn, side):
+        settle(ends[0].at[turn, pl.ds(side * half, half)], ends[2].at[side])
 
     def begin_apply(turn, vector):
         own_values[...] = vector
         for side in (sent_first, upper):
-            send_lists(turn, side, lists_of(turn, side))
-            if turn == 0 and side is sent_first:
-                pl.semaphore_wait(barrier, len(peers))
-            for k in range(half):
-                out_copy(turn, side, k).start()
+            for q in group_order:
+                list_values(turn, side, q)
+                if turn == 0 and side is sent_first and q == slow_group:
+                    pl.semaphore_wait(barrier, len(peers))
+                for k in block_order:
+                    if k // per_group == q:
+                        out_copy(turn, side, k).start()
 
     def apply(turn, vector, mixed, begin, middle):
         store(own_table, vector)
@@ -397,22 +406,30 @@
 
         lax.fori_loop(0, work_groups, take_own, 0, unroll=UNROLL)
 
-        finish(out_ends, turn, sent_first)
         early, late = sent_first, upper
-        lines = arrived(turn, early, mixed)
+        take_most(out_ends, turn, early)
+        take_slow(out_ends, turn, early)
+        lines = arrived(turn, early, mixed, range(half))
         base = own_rows + early * side_rows
         for g in range(work_groups):
             at = slice(8 * g, 8 * g + 8)
             cell_buf[at, :] = pick(lane_of[2 * turn, at, :], row_of[at, :] - base, lines, cell_buf[at, :])
 
-        finish(out_ends, turn, late)
-        lines = arrived(turn, late, mixed)
         base = own_rows + late * side_rows
+        if half > 1:
+            take_most(out_ends, turn, late)
+            lines = arrived(turn, late, mixed, block_order[1:])
+            for g in range(work_groups):
+                at = slice(8 * g, 8 * g + 8)
+                cell_buf[at, :] = pick(lane_of[2 * turn + 1, at, :], row_of[at, :] - base, lines, cell_buf[at, :])
+
+        take_slow(out_ends, turn, late)
+        lines = arrived(turn, late, mixed, [slow])
         resolved = []
         for h in range(con_rows):
             at, to = slice(8 * (con_base + h), 8 * (con_base + h) + 8), slice(8 * h, 8 * h + 8)
             found = pick(lane_of[2 * turn + 1, at, :], row_of[at, :] - base, lines, cell_buf[at, :])
-            resolved.append(jnp.sum(weights[to, :] * found, axis=0, keepdims=True))
+            resolved.append((h, jnp.sum(weights[to, :] * found, axis=0, keepdims=True)))
         found = []
         for g in range(cell_groups):
             at = slice(8 * g, 8 * g + 8)
@@ -434,13 +451,14 @@
         energy = energy + jnp.sum(weighted * vector, axis=0, keepdims=True)
         begin(energy)
 
-        far_acc[...] = jnp.zeros_like(far_acc)
-
-        def give_far(g, carry):
-            far_acc[...] += scatter_far(g, cell_buf[group(g), :])
-            return carry
-
-        lax.fori_loop(0, cell_groups, give_far, 0, unroll=8)
+
+        def give_all_far():
+            total = jnp.zeros((LANES, 2 * far_rows), jnp.float32)
+            for g in range(cell_groups):
+                total = total + scatter_far(g, cell_buf[8 * g : 8 * g + 8, :])
+            far_acc[...] = total
+
+        apart(give_all_far)
         total = jnp.transpose(far_acc[...])
         spread = total[0:ghost_rows] + total[ghost_rows : 2 * ghost_rows]
         summed = folded(total[2 * ghost_rows : 2 * far_rows])
@@ -452,7 +470,7 @@
             total = jnp.zeros((2 * ghost_rows, LANES), jnp.float32)
             for h in range(con_rows):
                 values = cell_buf[8 * (con_base + h) : 8 * (con_base + h) + 8, :]
-                total = total + scatter(con_base + h, values, own_rows, ghost_rows)
+                total = total + scatter(con_base + h, values, own_rows, ghost_rows, nodes)
             con_acc[...] = total
 
         apart(give_con)
@@ -460,7 +478,7 @@
         for j in range(blocks):
             back_src[turn, j] = spread[j * block_rows : (j + 1) * block_rows]
         for side in (late, early):
-            for k in range(half):
+            for k in block_order:
                 back_copy(turn, side, k).start()
         middle()
         own_acc[...] = jnp.zeros_like(own_acc)
@@ -470,18 +488,29 @@
             return carry
 
         lax.fori_loop(0, work_groups, give_own, 0, unroll=UNROLL)
-        for side in (late, early):
-            finish(back_ends, turn, side)
-
-            def give_list(side=side):
+        def give_lists(side, which):
+            def work():
                 both = own_acc[...]
-                for q in range(side_groups):
+                for q in which:
                     j = side * half + q * per_group
                     values = jnp.concatenate([back_dst[turn, j + r] for r in range(per_group)], axis=0)
                     both = both + scatter(list_base + side * side_groups + q, values, 0, own_rows)
                 own_acc[...] = both
 
-            apart(give_list)
+            apart(work)
+
+        sent(out_ends, turn, early)
+        sent(out_ends, turn, late)
+        take_most(back_ends, turn, late)
+        take_slow(back_ends, turn, late)
+        give_lists(late, group_order)
+        take_most(back_ends, turn, early)
+        if side_groups > 1:
+            give_lists(early, group_order[1:])
+        take_slow(back_ends, turn, early)
+        give_lists(early, group_order[:1])
+        sent(back_ends, turn, late)
+        sent(back_ends, turn, early)
         both = own_acc[...]
         return folded(both) + weighted
 
@@ -650,8 +679,8 @@
     ]
     exchange = pltpu.VMEM((ITERS, blocks, block_rows, LANES), jnp.float32)
     landing = pltpu.VMEM((ITERS + 1, blocks, block_rows, LANES), jnp.float32)
-    tile = jax.ShapeDtypeStruct((own_rows, LANES), jnp.float32)
-    line = jax.ShapeDtypeStruct((1, LANES), jnp.float32)
+    tile = pltpu.VMEM((own_rows, LANES), jnp.float32)
+    line = pltpu.VMEM((1, LANES), jnp.float32)
     answer, ahead, residual, applied, step = pl.pallas_call(
         functools.partial(kernel, shape, interp),
         out_shape=(tile, tile, tile, tile, line),
@@ -679,9 +708,9 @@
             pltpu.VMEM((ROUNDS, 1, LANES), jnp.float32),
             pltpu.VMEM((ROUNDS, far, 1, LANES), jnp.float32),
             pltpu.SemaphoreType.DMA((2,)),
+            pltpu.SemaphoreType.DMA((2, 2)),
             pltpu.SemaphoreType.DMA((2,)),
-            pltpu.SemaphoreType.DMA((2,)),
-            pltpu.SemaphoreType.DMA((2,)),
+            pltpu.SemaphoreType.DMA((2, 2)),
             pltpu.SemaphoreType.DMA((ROUNDS,)),
             pltpu.SemaphoreType.DMA((ROUNDS,)),
             pltpu.SemaphoreType.DMA((ROUNDS,)),

time: 46.9 us -> 43.3 us (0.923)
  Pallas kernels: 44 us -> 41.8 us
  other arithmetic: 1.47 us -> 0.67 us
  local copies, waits for them, and re-layouts: 0.62 us -> 0 us
    pallas_call x1, Pallas kernels: 44 us -> 41.8 us  [on_device(): pl.pallas_call(functools.partial(kernel, shape, interp), out_shape=(tile,...]
    reshape x1, other arithmetic: 1.47 us -> 0.67 us  [on_device(): (residual - scale * applied).reshape(own)]
    unnamed x2 -> x0, local copies, waits for them, and re-layouts: 0.62 us -> none
where the time goes in v2:
time: 43.3 us; the launch traced here: 43.1 us
  Pallas kernels  41.8 us (97%)
  other arithmetic  0.67 us (2%)
  between operations  0.64 us (1%)
    pallas_call x1, Pallas kernels, on_device(): pl.pallas_call(functools.partial(kernel, shape, interp), out_shape=(tile,...  41.8 us

profile of v2, /device:TPU:0, one launch (start us, length us, event | category | flops | bytes accessed | tf_op | source)
XLA Modules:
  0.0 43.1 jit_solution(9850192758504883783)
XLA Ops:
  0.6 41.8 %shard_map.95 = (f32[64,128]{1,0:T(8,128)S(1)}, f32[64,128]{1,0:T(8,128)S(1)}, f32[64,128]{1,0:T(8,128)S(1)}, f32[64,128]{1,0:T(8,128)S(1)}, f32[1,128]{1,0:T(1,128)S(1)}) custom-call(f32[64,128]{1,0:T(8,128)} %bitcast.11, f32[64,128]{1,0:T(8,128)} %bitcast.12, s32[125,128]{1,0:T(8,128)} %refs_2_.1, s32[1,128]{1,0:T(1,128)} %bitcast.14, s32[5,256]{1,0:T(8,128)} %refs_4_.1, ...), custom_call_target="tpu_custom_call" | custom-call | tf_op jit(solution)/shard_map/pallas_call | solution.py:684
  42.4 0.7 %subtract_bitcast_fusion = (f32[8192]{0:T(1024)}, f32[8192]{0:T(1024)}) fusion(f32[64,128]{1,0:T(8,128)S(1)} %get-tuple-element.10, f32[64,128]{1,0:T(8,128)S(1)} %get-tuple-element.11, f32[]{:T(128)S(1)} %bitcast.10, f32[64,128]{1,0:T(8,128)S(1)} %get-tuple-element.7, f32[64,128]{1,0:T(8,128)S(1)} %get-tuple-element.9), kind=kLoop, calls=%fused_computation | loop fusion | flops 32768 | bytes 196612 | tf_op jit(solution)/shard_map/reshape | solution.py:726

commit v3 on v2

--- a/solution.py
+++ b/solution.py
@@ -172,7 +172,9 @@
         return lax.rem(me + distance + count, count)
 
     barrier = pltpu.get_barrier_semaphore()
-    peers = [ring_peer(offset(side, k)) for side in range(2) for k in range(half)]
+    peers = []
+    if far > 1:
+        peers += [ring_peer(offset(side, k)) for side in range(2) for k in range(half)]
     peers += [near_peer(step) for step in range(1, near)]
     peers += [far_peer(step) for step in range(1, far)]
     for peer in peers:
@@ -248,25 +250,25 @@
         high = values.astype(jnp.bfloat16).astype(jnp.float32)
         return high, values - high
 
-    def against(placed, g):
+    def against(placed, g, first):
         return lax.dot_general(
             placed,
-            onehot[g, :, 0 : placed.shape[1]],
+            onehot[g, :, first * LANES : first * LANES + placed.shape[1]],
             (((1,), (1,)), ((), ())),
             preferred_element_type=jnp.float32,
         )
 
-    def scatter(g, values, base, depth, count=8):
+    def scatter(g, values, base, depth, first=0):
         rows = row_of[group(g), :] - base
         high, low = parts_of(values)
         row_iota = lax.broadcasted_iota(jnp.int32, (depth, LANES), 0)
         columns = []
-        for i in range(count):
-            hit = rows[i : i + 1, :] == row_iota
+        for i in range(values.shape[0]):
+            hit = rows[first + i : first + i + 1, :] == row_iota
             upper_part = jnp.where(hit, high[i : i + 1, :], 0.0).astype(jnp.bfloat16)
             lower_part = jnp.where(hit, low[i : i + 1, :], 0.0).astype(jnp.bfloat16)
             columns.append(jnp.concatenate([upper_part, lower_part], axis=0))
-        return against(jnp.concatenate(columns, axis=1), g)
+        return against(jnp.concatenate(columns, axis=1), g, first)
 
     def scatter_far(g, values):
         rows = row_of[group(g), :] - own_rows
@@ -433,11 +435,9 @@
         found = []
         for g in range(cell_groups):
             at = slice(8 * g, 8 * g + 8)
-            found.append(pick(lane_of[2 * turn + 1, at, :], row_of[at, :] - base, lines, cell_buf[at, :]))
-        for g in range(cell_groups):
-            at = slice(8 * g, 8 * g + 8)
-            rows = row_of[at, :] - (own_rows + ghost_rows)
-            found[g] = pick(lane_of[2 * turn + 1, at, :], rows, resolved, found[g])
+            lanes, rows = lane_of[2 * turn + 1, at, :], row_of[at, :]
+            part_found = pick(lanes, rows - base, lines, cell_buf[at, :])
+            found.append(pick(lanes, rows - (own_rows + ghost_rows), resolved, part_found))
         nodal = jnp.concatenate(found, axis=0)
         contrib = scale * jnp.dot(
             stiff_ref[...],
@@ -469,8 +469,8 @@
         def give_con():
             total = jnp.zeros((2 * ghost_rows, LANES), jnp.float32)
             for h in range(con_rows):
-                values = cell_buf[8 * (con_base + h) : 8 * (con_base + h) + 8, :]
-                total = total + scatter(con_base + h, values, own_rows, ghost_rows, nodes)
+                values = cell_buf[8 * (con_base + h) : 8 * (con_base + h) + nodes, :]
+                total = total + scatter(con_base + h, values, own_rows, ghost_rows)
             con_acc[...] = total
 
         apart(give_con)
@@ -491,10 +491,13 @@
         def give_lists(side, which):
             def work():
                 both = own_acc[...]
-                for q in which:
-                    j = side * half + q * per_group
-                    values = jnp.concatenate([back_dst[turn, j + r] for r in range(per_group)], axis=0)
-                    both = both + scatter(list_base + side * side_groups + q, values, 0, own_rows)
+                for q in range(side_groups):
+                    chosen = [k for k in which if k // per_group == q]
+                    if not chosen:
+                        continue
+                    values = jnp.concatenate([back_dst[turn, side * half + k] for k in chosen], axis=0)
+                    first = (chosen[0] - q * per_group) * block_rows
+                    both = both + scatter(list_base + side * side_groups + q, values, 0, own_rows, first)
                 own_acc[...] = both
 
             apart(work)
@@ -503,12 +506,12 @@
         sent(out_ends, turn, late)
         take_most(back_ends, turn, late)
         take_slow(back_ends, turn, late)
-        give_lists(late, group_order)
+        give_lists(late, range(half))
         take_most(back_ends, turn, early)
-        if side_groups > 1:
-            give_lists(early, group_order[1:])
+        if half > 1:
+            give_lists(early, sorted(block_order[1:]))
         take_slow(back_ends, turn, early)
-        give_lists(early, group_order[:1])
+        give_lists(early, [slow])
         sent(back_ends, turn, late)
         sent(back_ends, turn, early)
         both = own_acc[...]

time: 43.3 us -> 43.1 us (level)
  no operation moved by 1% of the time
where the time goes in v3:
time: 43.1 us; the launch traced here: 42.9 us
  Pallas kernels  41.6 us (97%)
  other arithmetic  0.67 us (2%)
  between operations  0.64 us (1%)
    pallas_call x1, Pallas kernels, on_device(): pl.pallas_call(functools.partial(kernel, shape, interp), out_shape=(tile,...  41.6 us

profile of v3, /device:TPU:0, one launch (start us, length us, event | category | flops | bytes accessed | tf_op | source)
XLA Modules:
  0.0 42.9 jit_solution(5277337943951049792)
XLA Ops:
  0.6 41.6 %shard_map.95 = (f32[64,128]{1,0:T(8,128)S(1)}, f32[64,128]{1,0:T(8,128)S(1)}, f32[64,128]{1,0:T(8,128)S(1)}, f32[64,128]{1,0:T(8,128)S(1)}, f32[1,128]{1,0:T(1,128)S(1)}) custom-call(f32[64,128]{1,0:T(8,128)} %bitcast.11, f32[64,128]{1,0:T(8,128)} %bitcast.12, s32[125,128]{1,0:T(8,128)} %refs_2_.1, s32[1,128]{1,0:T(1,128)} %bitcast.14, s32[5,256]{1,0:T(8,128)} %refs_4_.1, ...), custom_call_target="tpu_custom_call" | custom-call | tf_op jit(solution)/shard_map/pallas_call | solution.py:687
  42.3 0.7 %subtract_bitcast_fusion = (f32[8192]{0:T(1024)}, f32[8192]{0:T(1024)}) fusion(f32[64,128]{1,0:T(8,128)S(1)} %get-tuple-element.10, f32[64,128]{1,0:T(8,128)S(1)} %get-tuple-element.11, f32[]{:T(128)S(1)} %bitcast.10, f32[64,128]{1,0:T(8,128)S(1)} %get-tuple-element.7, f32[64,128]{1,0:T(8,128)S(1)} %get-tuple-element.9), kind=kLoop, calls=%fused_computation | loop fusion | flops 32768 | bytes 196612 | tf_op jit(solution)/shard_map/reshape | solution.py:729

commit v4 on v3

--- a/solution.py
+++ b/solution.py
@@ -399,7 +399,7 @@
                     if k // per_group == q:
                         out_copy(turn, side, k).start()
 
-    def apply(turn, vector, mixed, begin, middle):
+    def apply(turn, vector, mixed, begin, middle, ready=lambda: None):
         store(own_table, vector)
 
         def take_own(g, carry):
@@ -433,11 +433,17 @@
             found = pick(lane_of[2 * turn + 1, at, :], row_of[at, :] - base, lines, cell_buf[at, :])
             resolved.append((h, jnp.sum(weights[to, :] * found, axis=0, keepdims=True)))
         found = []
+        ahead = min(4, cell_groups)
         for g in range(cell_groups):
             at = slice(8 * g, 8 * g + 8)
             lanes, rows = lane_of[2 * turn + 1, at, :], row_of[at, :]
-            part_found = pick(lanes, rows - base, lines, cell_buf[at, :])
-            found.append(pick(lanes, rows - (own_rows + ghost_rows), resolved, part_found))
+            found.append(pick(lanes, rows - base, lines, cell_buf[at, :]))
+            if g >= ahead:
+                found[g] = pick(lanes, rows - (own_rows + ghost_rows), resolved, found[g])
+        for g in range(ahead):
+            at = slice(8 * g, 8 * g + 8)
+            lanes, rows = lane_of[2 * turn + 1, at, :], row_of[at, :]
+            found[g] = pick(lanes, rows - (own_rows + ghost_rows), resolved, found[g])
         nodal = jnp.concatenate(found, axis=0)
         contrib = scale * jnp.dot(
             stiff_ref[...],
@@ -510,6 +516,7 @@
         take_most(back_ends, turn, early)
         if half > 1:
             give_lists(early, sorted(block_order[1:]))
+        ready()
         take_slow(back_ends, turn, early)
         give_lists(early, [slow])
         sent(back_ends, turn, late)
@@ -629,16 +636,22 @@
     direction = before + ratio1 * start
     answer = step0 * start + step1 * direction
     square = dot(residual, residual)
+    scalars = []
+
+    def last_sums():
+        norm2, product2, unused_a, unused_b = sums_end(1)
+        ratio2 = norm2 / norm1
+        scalars.extend([ratio2, norm2 / (product2 - ratio2 * norm2 / step1)])
+
     applied = apply(
         2,
         residual,
         lambda *held: next_residual(*held)[2],
         lambda energy: sums_start(1, [square, energy]),
         lambda: sums_middle(1),
+        last_sums,
     )
-    norm2, product2, unused_a, unused_b = sums_end(1)
-    ratio2 = norm2 / norm1
-    step2 = norm2 / (product2 - ratio2 * norm2 / step1)
+    ratio2, step2 = scalars
     answer_ref[...] = answer
     ahead_ref[...] = residual + ratio2 * direction
     residual_ref[...] = residual
@@ -716,8 +729,8 @@
             pltpu.SemaphoreType.DMA((2, 2)),
             pltpu.SemaphoreType.DMA((ROUNDS,)),
             pltpu.SemaphoreType.DMA((ROUNDS,)),
-            pltpu.SemaphoreType.DMA((ROUNDS,)),
-            pltpu.SemaphoreType.DMA((ROUNDS,)),
+            pltpu.SemaphoreType.DMA((ROUNDS if far > 1 else 1,)),
+            pltpu.SemaphoreType.DMA((ROUNDS if far > 1 else 1,)),
         ],
         compiler_params=pltpu.CompilerParams(
             collective_id=0, has_side_effects=True, vmem_limit_bytes=60 * 1024 * 1024

time: 43.1 us -> 43.2 us (level)
  no operation moved by 1% of the time
where the time goes in v4:
time: 43.2 us; the launch traced here: 43 us
  Pallas kernels  41.7 us (97%)
  other arithmetic  0.67 us (2%)
  between operations  0.64 us (1%)
    pallas_call x1, Pallas kernels, on_device(): pl.pallas_call(functools.partial(kernel, shape, interp), out_shape=(tile,...  41.7 us

profile of v4, /device:TPU:0, one launch (start us, length us, event | category | flops | bytes accessed | tf_op | source)
XLA Modules:
  0.0 43.0 jit_solution(15254748053414297096)
XLA Ops:
  0.6 41.7 %shard_map.95 = (f32[64,128]{1,0:T(8,128)S(1)}, f32[64,128]{1,0:T(8,128)S(1)}, f32[64,128]{1,0:T(8,128)S(1)}, f32[64,128]{1,0:T(8,128)S(1)}, f32[1,128]{1,0:T(1,128)S(1)}) custom-call(f32[64,128]{1,0:T(8,128)} %bitcast.11, f32[64,128]{1,0:T(8,128)} %bitcast.12, s32[125,128]{1,0:T(8,128)} %refs_2_.1, s32[1,128]{1,0:T(1,128)} %bitcast.14, s32[5,256]{1,0:T(8,128)} %refs_4_.1, ...), custom_call_target="tpu_custom_call" | custom-call | tf_op jit(solution)/shard_map/pallas_call | solution.py:700
  42.4 0.7 %subtract_bitcast_fusion = (f32[8192]{0:T(1024)}, f32[8192]{0:T(1024)}) fusion(f32[64,128]{1,0:T(8,128)S(1)} %get-tuple-element.10, f32[64,128]{1,0:T(8,128)S(1)} %get-tuple-element.11, f32[]{:T(128)S(1)} %bitcast.10, f32[64,128]{1,0:T(8,128)S(1)} %get-tuple-element.7, f32[64,128]{1,0:T(8,128)S(1)} %get-tuple-element.9), kind=kLoop, calls=%fused_computation | loop fusion | flops 32768 | bytes 196612 | tf_op jit(solution)/shard_map/reshape | solution.py:742
